TPU v7x, 32 devices: a whole 2x2x4 slice. The times are simulated.
32 devices in a mesh: grp: 2 (over y), gy: 4 (over z), gx: 2 (over x), gz: 2 (over core).
Axes of the slice: x: 2, y: 2, z: 4, core: 2. Of those that a mesh axis runs over, the one named last changes fastest.
Arguments:
- pair: bfloat16 [1024, 512, 128], P(('grp', 'gx', 'gz'), 'gy'), parts along dimension 0, may hold values from -6 to 6
- lengths: int32 [2], P('grp'), parts along dimension 0, may hold values from 256 to 512
- ln_gain: float32 [128], replicated, may hold values from 0.1 to 1.9
- ln_bias: float32 [128], replicated, may hold values from -3 to 3
- w_ab: bfloat16 [128, 512], replicated, may hold values from -0.5 to 0.5
- w_gate: bfloat16 [128, 128], replicated, may hold values from -0.5 to 0.5
- out_gain: float32 [128], replicated, may hold values from 0.1 to 1.9
- out_bias: float32 [128], replicated, may hold values from -3 to 3
- w_out: bfloat16 [128, 128], replicated, may hold values from -0.5 to 0.5
Outputs:
- update: bfloat16 [1024, 512, 128], P(('grp', 'gx', 'gz'), 'gy'), parts along dimension 0
There are 2 independent parts, one for each index of `grp`. A program takes and returns all parts, laid end to end along the dimension named above; an argument that names none is the same for every part. Nothing has to cross between parts.
Inputs may be any that keep to these rules, and one draw needn't show every extreme that they name: Residues from lengths[0] on are padding.
All inputs are finite; a program needn't handle non-finite values.
Results may differ from a plain program's by a relative error of at most 0.0052.
Values may be sent and summed in bfloat16 or wider, within the bound.
A program may use at most 128 MiB of HBM per device.

v0:
```python
import functools

import jax
import jax.numpy as jnp
from jax import lax
from jax.experimental import pallas as pl
from jax.experimental.pallas import tpu as pltpu
from jax.sharding import PartitionSpec as P

CHUNKS = 32
LAG = 2
DIRECT = 2
GROUPS = 4
ROWS = 32


def layer_norm(values, gain, bias):
    values = values.astype(jnp.float32)
    mean = jnp.mean(values, -1, keepdims=True)
    spread = jnp.mean(jnp.square(values - mean), -1, keepdims=True)
    return (values - mean) * lax.rsqrt(spread + 1e-05) * gain + bias


def channel_norm(values, gain, bias):
    mean = jnp.mean(values, 0, keepdims=True)
    spread = jnp.mean(jnp.square(values - mean), 0, keepdims=True)
    return (values - mean) * lax.rsqrt(spread + 1e-05) * gain[:, None, None] + bias[:, None, None]


def gather_body(pair, lengths, ln_gain, ln_bias, w_ab, w_gate, out_gain, out_bias, w_out):
    tile_rows, tile_cols, width = pair.shape
    hidden = w_out.shape[0]
    row_start = lax.axis_index(("gx", "gz")) * tile_rows
    col_index = lax.axis_index("gy")
    col_start = col_index * tile_cols
    normed = layer_norm(pair, ln_gain, ln_bias).astype(jnp.bfloat16)
    flat = normed.reshape(tile_rows * tile_cols, width)
    proj = jnp.dot(flat, w_ab, preferred_element_type=jnp.float32).reshape(
        tile_rows, tile_cols, 4 * hidden
    )
    row_live = (row_start + jnp.arange(tile_rows, dtype=jnp.int32) < lengths[0]).astype(jnp.float32)
    col_live = (col_start + jnp.arange(tile_cols, dtype=jnp.int32) < lengths[0]).astype(jnp.float32)
    pair_mask = (row_live[:, None] * col_live[None, :])[..., None]
    left = (pair_mask * jax.nn.sigmoid(proj[..., :hidden]) * proj[..., hidden : 2 * hidden]).astype(
        jnp.bfloat16
    )
    right = (
        pair_mask * jax.nn.sigmoid(proj[..., 2 * hidden : 3 * hidden]) * proj[..., 3 * hidden :]
    ).astype(jnp.bfloat16)
    left_major = jnp.transpose(left, (2, 0, 1))
    right_major = jnp.transpose(right, (2, 0, 1))
    column_rows = lax.all_gather(right_major, ("gx", "gz"), axis=1, tiled=True)
    right_mine = lax.all_to_all(column_rows, "gy", split_axis=1, concat_axis=2, tiled=True)
    triangle = jnp.einsum(
        "cik,cjk->cij",
        lax.all_gather(left_major, "gy", axis=2, tiled=True),
        right_mine,
        preferred_element_type=jnp.float32,
    )
    tri_norm = channel_norm(triangle, out_gain, out_bias).astype(jnp.bfloat16)
    gate = jax.nn.sigmoid(jnp.dot(flat, w_gate, preferred_element_type=jnp.float32)).reshape(
        tile_rows, tile_cols, width
    )
    projected = jnp.einsum("cij,cd->ijd", tri_norm, w_out, preferred_element_type=jnp.float32)
    return (gate * projected).astype(jnp.bfloat16)


def exchange_kernel(
    nx,
    nz,
    lengths,
    pair,
    gain,
    bias,
    w_ab,
    w_gate,
    out,
    gate_out,
    normed,
    send,
    gate_held,
    held,
    given,
    taken,
    deal_send,
    deal_recv,
    pass_send,
    pass_recv,
    cross_send,
    cross_recv,
    back_send,
    back_recv,
    own_sem,
    pair_sem,
    gate_sem,
    direct_send,
    direct_recv,
):
    nr = nx * nz
    hidden, rows, cols = send.shape[1:]
    width = pair.shape[2]
    blocks, lanes = rows // ROWS, ROWS * cols
    each = hidden // nr
    chunks = pass_send.shape[0]
    part = each // chunks
    gy, gx, gz = lax.axis_index("gy"), lax.axis_index("gx"), lax.axis_index("gz")
    me = gx * nz + gz
    half = gy // 2
    inner_plane, outer_plane = 1 + half, 3 * half
    inner = gy == inner_plane
    outer = jnp.logical_not(inner)

    def place(tall, plane):
        return {"gy": plane, "gx": tall // nz, "gz": tall % nz}

    def remote(src, dst, send_sem, recv_sem, device):
        return pltpu.make_async_remote_copy(
            src_ref=src,
            dst_ref=dst,
            send_sem=send_sem,
            recv_sem=recv_sem,
            device_id=device,
            device_id_type=pl.DeviceIdType.MESH,
        )

    def channels(chunk):
        return pl.ds(chunk * part, part)

    def band(tall):
        return pl.ds(pl.multiple_of(tall * rows, rows), rows)

    def columns(plane):
        return pl.ds(pl.multiple_of((plane - 2 * half) * cols, cols), cols)

    def deal(chunk, step):
        peer = lax.rem(me + step, nr)
        return remote(
            send.at[:, pl.ds(peer * each + chunk * part, part)],
            held.at[:, channels(chunk), band(me), pl.ds(0, cols)],
            deal_send.at[chunk, step],
            deal_recv.at[chunk, step],
            place(peer, gy),
        )

    def keep_in(chunk):
        return pltpu.make_async_copy(
            send.at[:, pl.ds(me * each + chunk * part, part)],
            held.at[:, channels(chunk), band(me), pl.ds(0, cols)],
            own_sem.at[0, chunk],
        )

    def pass_on(chunk):
        return remote(
            held.at[:, channels(chunk), :, pl.ds(0, cols)],
            held.at[:, channels(chunk), :, pl.ds(cols, cols)],
            pass_send.at[chunk],
            pass_recv.at[chunk],
            place(me, inner_plane),
        )

    def deal_inward(chunk, step):
        peer = lax.rem(me + step, nr)
        return remote(
            send.at[:, pl.ds(peer * each + chunk * part, part)],
            held.at[:, channels(chunk), band(me), pl.ds(cols, cols)],
            direct_send.at[chunk, step],
            direct_recv.at[chunk, step],
            place(peer, inner_plane),
        )

    def cross(chunk):
        return remote(
            given.at[channels(chunk)],
            taken.at[channels(chunk)],
            cross_send.at[chunk],
            cross_recv.at[chunk],
            place(me, 3 - gy),
        )

    def hand_back(chunk, step, plane, side):
        peer = lax.rem(me + step, nr)
        return remote(
            taken.at[channels(chunk), band(peer), columns(plane)],
            out.at[pl.ds(me * each + chunk * part, part)],
            back_send.at[side, chunk, step],
            back_recv.at[chunk, step],
            place(peer, plane),
        )

    def keep_out(chunk):
        return pltpu.make_async_copy(
            taken.at[channels(chunk), band(me), columns(inner_plane)],
            out.at[pl.ds(me * each + chunk * part, part)],
            own_sem.at[1, chunk],
        )

    def load(block):
        return pltpu.make_async_copy(
            pair.at[pl.ds(block * ROWS, ROWS)],
            normed.at[pl.ds(block * ROWS, ROWS)],
            pair_sem.at[block],
        )

    for block in range(blocks):
        load(block).start()
    barrier = pltpu.get_barrier_semaphore()
    total = 4 * nr
    index = gy * nr + me
    for step in range(1, total):
        peer = lax.rem(index + step, total)
        pl.semaphore_signal(
            barrier,
            inc=1,
            device_id=place(peer % nr, peer // nr),
            device_id_type=pl.DeviceIdType.MESH,
        )
    def dealt(chunk):
        for step in range(1, nr):
            deal(chunk, step).wait_recv()
        keep_in(chunk).wait()

    def product(channel, which):
        below = pl.ds(pl.multiple_of(which * 2 * cols, 2 * cols), 2 * cols)
        return lax.dot_general(
            held[0, channel],
            held[1, channel, below, :],
            (((1,), (1,)), ((), ())),
            preferred_element_type=jnp.float32,
        )

    @pl.loop(0, blocks)
    def _(block):
        load(block).wait()
        here = pl.ds(pl.multiple_of(block * ROWS, ROWS), ROWS)
        flat = normed[here].reshape(lanes, width)
        value = layer_norm(flat, gain[...], bias[...]).astype(jnp.bfloat16)
        normed[here] = value.reshape(ROWS, cols, width)

    upright_w = jnp.transpose(w_ab[...].astype(jnp.float32))
    lane = lax.broadcasted_iota(jnp.int32, (1, lanes), 1)
    col_live = gy * cols + lane % cols < lengths[0]
    span = each // GROUPS

    def project(group):
        starts = [
            kind * hidden + tall * each + group * span for kind in range(4) for tall in range(nr)
        ]
        weights = jnp.concatenate([upright_w[at : at + span] for at in starts]).astype(jnp.bfloat16)
        height = nr * span

        @pl.loop(0, blocks)
        def _(block):
            here = pl.ds(pl.multiple_of(block * ROWS, ROWS), ROWS)
            proj = lax.dot_general(
                weights,
                normed[here].reshape(lanes, width),
                (((1,), (1,)), ((), ())),
                preferred_element_type=jnp.float32,
            )
            row_live = me * rows + block * ROWS + lane // cols < lengths[0]
            mask = (row_live & col_live).astype(jnp.float32)
            for side in range(2):
                gates = proj[2 * side * height : (2 * side + 1) * height]
                values = proj[(2 * side + 1) * height : (2 * side + 2) * height]
                value = mask * jax.nn.sigmoid(gates) * values
                value = value.reshape(height, ROWS, cols).astype(jnp.bfloat16)
                for tall in range(nr):
                    first = tall * each + group * span
                    send[side, first : first + span, here] = value[tall * span : (tall + 1) * span]

        if group == 0:
            pl.semaphore_wait(barrier, total - 1)

        @pl.loop(group * span // part, (group + 1) * span // part)
        def _(chunk):
            direct = outer & (chunk < DIRECT)

            @pl.when(direct)
            def _():
                for step in range(nr):
                    deal_inward(chunk, step).start()

            @pl.when(jnp.logical_not(direct))
            def _():
                for step in range(1, nr):
                    deal(chunk, step).start()
                keep_in(chunk).start()

    for group in range(GROUPS):
        project(group)
        if group:

            @pl.when(outer)
            def _():
                dealt(DIRECT + group - 1)
                pass_on(DIRECT + group - 1).start()

    def store_gate(block):
        return pltpu.make_async_copy(
            gate_held.at[block % 2],
            gate_out.at[pl.ds(block * ROWS, ROWS)],
            gate_sem.at[block % 2],
        )

    def gate_turn(turn):
        block = turn - 2 * GROUPS

        @pl.when((block >= 2) & (block < blocks + 2))
        def _():
            store_gate(block - 2).wait()

        @pl.when((block >= 0) & (block < blocks))
        def _():
            here = pl.ds(pl.multiple_of(block * ROWS, ROWS), ROWS)
            value = jax.nn.sigmoid(
                jnp.dot(
                    normed[here].reshape(lanes, width),
                    w_gate[...],
                    preferred_element_type=jnp.float32,
                )
            )
            gate_held[block % 2] = value.reshape(ROWS, cols, width)
            store_gate(block).start()

    @pl.when(outer)
    def _():
        @pl.loop(DIRECT + GROUPS - 1, chunks)
        def _(chunk):
            dealt(chunk)
            pass_on(chunk).start()
            gate_turn(chunk)

        @pl.loop(0, chunks)
        def _(chunk):
            for step in range(nr):
                hand_back(chunk, step, outer_plane, 1).wait_recv()

            @pl.when(chunk < DIRECT)
            def _():
                for step in range(nr):
                    deal_inward(chunk, step).wait_send()

            @pl.when(chunk >= DIRECT)
            def _():
                for step in range(1, nr):
                    deal(chunk, step).wait_send()
                pass_on(chunk).wait_send()

    @pl.when(inner)
    def _():
        @pl.loop(0, chunks + LAG)
        def _(turn):
            @pl.when(turn < chunks)
            def _():
                dealt(turn)

                @pl.when(turn < DIRECT)
                def _():
                    for step in range(nr):
                        deal_inward(turn, step).wait_recv()

                @pl.when(turn >= DIRECT)
                def _():
                    pass_on(turn).wait_recv()


                @pl.loop(turn * part, (turn + 1) * part)
                def _(channel):
                    given[channel] = product(channel, 1 - half).astype(jnp.bfloat16)

                cross(turn).start()

            @pl.when(turn >= LAG)
            def _():
                chunk = turn - LAG
                cross(chunk).wait_recv()

                @pl.loop(chunk * part, (chunk + 1) * part)
                def _(channel):
                    total = product(channel, half) + taken[channel].astype(jnp.float32)
                    taken[channel] = total.astype(jnp.bfloat16)

                for step in range(nr):
                    hand_back(chunk, step, outer_plane, 1).start()
                for step in range(1, nr):
                    hand_back(chunk, step, inner_plane, 0).start()
                keep_out(chunk).start()

            gate_turn(turn)

        @pl.loop(0, chunks)
        def _(chunk):
            for step in range(1, nr):
                hand_back(chunk, step, inner_plane, 0).wait_recv()
                hand_back(chunk, step, inner_plane, 0).wait_send()
                deal(chunk, step).wait_send()
            for step in range(nr):
                hand_back(chunk, step, outer_plane, 1).wait_send()
            cross(chunk).wait_send()
            keep_out(chunk).wait()


def upright(row):
    return jnp.transpose(jnp.broadcast_to(row[...], (row.shape[1], row.shape[1])))[:, :1]


def finish_kernel(gate, tri, out_gain, out_bias, w_out, out):
    rows, cols, width = out.shape
    hidden = tri.shape[0]
    values = tri[...].astype(jnp.float32)
    mean = jnp.mean(values, 0, keepdims=True)
    centred = values - mean
    spread = jnp.mean(jnp.square(centred), 0, keepdims=True)
    scaled = (centred * lax.rsqrt(spread + 1e-05)).reshape(hidden, rows * cols)
    tri_norm = (scaled * upright(out_gain) + upright(out_bias)).astype(jnp.bfloat16)
    projected = lax.dot_general(
        tri_norm, w_out[...], (((0,), (0,)), ((), ())), preferred_element_type=jnp.float32
    )
    out[...] = (gate[...] * projected.reshape(rows, cols, width)).astype(jnp.bfloat16)


def whole(shape):
    return pl.BlockSpec(shape, lambda step: (0,) * len(shape))


def channel_body(sizes, pair, lengths, ln_gain, ln_bias, w_ab, w_gate, out_gain, out_bias, w_out):
    ny, nx, nz = sizes
    tile_rows, tile_cols, width = pair.shape
    hidden = w_out.shape[0]
    gain, bias = ln_gain[None, :], ln_bias[None, :]
    smem = pl.BlockSpec(memory_space=pltpu.SMEM)
    steps = tile_rows // ROWS
    dma = pltpu.SemaphoreType.DMA
    any_space = pl.BlockSpec(memory_space=pl.ANY)
    nr = nx * nz
    each, side = hidden // nr, nr * tile_rows
    vmem = pl.BlockSpec(memory_space=pltpu.VMEM)
    triangle, gate = pl.pallas_call(
        functools.partial(exchange_kernel, nx, nz),
        name="exchange",
        out_shape=(
            jax.ShapeDtypeStruct((hidden, tile_rows, tile_cols), jnp.bfloat16),
            jax.ShapeDtypeStruct(pair.shape, jnp.float32),
        ),
        in_specs=[smem, any_space, vmem, vmem, vmem, vmem],
        out_specs=(any_space, any_space),
        scratch_shapes=[
            pltpu.VMEM(pair.shape, jnp.bfloat16),
            pltpu.VMEM((2, hidden, tile_rows, tile_cols), jnp.bfloat16),
            pltpu.VMEM((2, ROWS, tile_cols, width), jnp.float32),
            pltpu.VMEM((2, each, side, 2 * tile_cols), jnp.bfloat16),
            pltpu.VMEM((each, side, 2 * tile_cols), jnp.bfloat16),
            pltpu.VMEM((each, side, 2 * tile_cols), jnp.bfloat16),
            dma((CHUNKS, nr)),
            dma((CHUNKS, nr)),
            dma((CHUNKS,)),
            dma((CHUNKS,)),
            dma((CHUNKS,)),
            dma((CHUNKS,)),
            dma((2, CHUNKS, nr)),
            dma((CHUNKS, nr)),
            dma((2, CHUNKS)),
            dma((steps,)),
            dma((2,)),
            dma((DIRECT, nr)),
            dma((DIRECT, nr)),
        ],
        compiler_params=pltpu.CompilerParams(
            collective_id=0, has_side_effects=True, vmem_limit_bytes=63 * 2**20
        ),
    )(lengths, pair, gain, bias, w_ab, w_gate)
    return pl.pallas_call(
        finish_kernel,
        name="finish",
        grid=(steps,),
        out_shape=jax.ShapeDtypeStruct(pair.shape, jnp.bfloat16),
        in_specs=[
            pl.BlockSpec((ROWS, tile_cols, width), lambda step: (step, 0, 0)),
            pl.BlockSpec((hidden, ROWS, tile_cols), lambda step: (0, step, 0)),
            whole((1, hidden)),
            whole((1, hidden)),
            whole((hidden, width)),
        ],
        out_specs=pl.BlockSpec((ROWS, tile_cols, width), lambda step: (step, 0, 0)),
        compiler_params=pltpu.CompilerParams(vmem_limit_bytes=56 * 2**20),
    )(gate, triangle, out_gain[None, :], out_bias[None, :], w_out)


def body(sizes, pair, *rest):
    ny, nx, nz = sizes
    hidden = rest[-1].shape[0]
    tile_rows, tile_cols, _ = pair.shape
    fits = (
        ny == 4
        and hidden % (nx * nz * CHUNKS) == 0
        and hidden % (nx * nz * GROUPS * 8) == 0
        and nx * nz * tile_rows == ny * tile_cols
        and tile_rows % ROWS == 0
        and tile_cols % 128 == 0
        and 2 * 5 * hidden * tile_rows * tile_cols * 2 <= 48 * 2**20
    )
    return channel_body(sizes, pair, *rest) if fits else gather_body(pair, *rest)


def solution(mesh):
    in_specs = (P(("grp", "gx", "gz"), "gy", None), P("grp"), P(), P(), P(), P(), P(), P(), P())
    out_specs = P(("grp", "gx", "gz"), "gy", None)
    sizes = (mesh.shape["gy"], mesh.shape["gx"], mesh.shape["gz"])
    return jax.shard_map(
        functools.partial(body, sizes), mesh=mesh, in_specs=in_specs, out_specs=out_specs, check_vma=False
    )
```

profile of v0, /device:TPU:0, one launch (start us, length us, event | category | flops | bytes accessed | tf_op | source)
XLA Modules:
  0.0 226.8 jit_solution(11636215951375854526)
XLA Ops:
  0.7 215.9 %exchange.1 = (bf16[128,128,128]{2,1,0:T(8,128)(2,1)}, f32[128,128,128]{2,1,0:T(8,128)}) custom-call(s32[1]{0:T(128)S(6)} %copy.10.lengths, bf16[128,128,128]{2,1,0:T(8,128)(2,1)} %pair.1, f32[1,128]{1,0:T(1,128)} %bitcast.4, f32[1,128]{1,0:T(1,128)} %bitcast.5, bf16[128,512]{1,0:T(8,128)(2,1)} %w_ab.1, bf16[128,128]{1,0:T(8,128)(2,1)} %w_gate.1), custom_call_target="tpu_custom_call" | custom-call | tf_op jit(solution)/shard_map/exchange/pallas_call | solution.py:438
  216.5 10.3 %finish.1 = bf16[128,128,128]{2,1,0:T(8,128)(2,1)} custom-call(f32[128,128,128]{2,1,0:T(8,128)} %get-tuple-element.7.gate, bf16[128,128,128]{2,1,0:T(8,128)(2,1)} %get-tuple-element.8.tri, f32[1,128]{1,0:T(1,128)} %bitcast.6, f32[1,128]{1,0:T(1,128)} %bitcast.7, bf16[128,128]{1,0:T(8,128)(2,1)} %w_out.1), custom_call_target="tpu_custom_call" | custom-call | tf_op jit(solution)/shard_map/finish/pallas_call | solution.py:472
where the time goes:
time: 227 us
  Pallas kernels  226 us (100%)
    pallas_call x1, Pallas kernels, channel_body(): pl.pallas_call(functools.partial(exchange_kernel, nx, nz), name='exchange...  216 us
    pallas_call x1, Pallas kernels, channel_body(): pl.pallas_call(finish_kernel, name='finish', grid=(steps,), out_shape=jax...  10.3 us

commit v1 on v0

--- a/solution.py
+++ b/solution.py
@@ -82,26 +82,22 @@
     held,
     given,
     taken,
-    deal_send,
-    deal_recv,
+    operand_send,
+    operand_recv,
     pass_send,
-    pass_recv,
     cross_send,
     cross_recv,
     back_send,
     back_recv,
-    own_sem,
     pair_sem,
     gate_sem,
-    direct_send,
-    direct_recv,
 ):
     nr = nx * nz
     hidden, rows, cols = send.shape[1:]
     width = pair.shape[2]
     blocks, lanes = rows // ROWS, ROWS * cols
     each = hidden // nr
-    chunks = pass_send.shape[0]
+    chunks = cross_recv.shape[0]
     part = each // chunks
     gy, gx, gz = lax.axis_index("gy"), lax.axis_index("gx"), lax.axis_index("gz")
     me = gx * nz + gz
@@ -137,8 +133,8 @@
         return remote(
             send.at[:, pl.ds(peer * each + chunk * part, part)],
             held.at[:, channels(chunk), band(me), pl.ds(0, cols)],
-            deal_send.at[chunk, step],
-            deal_recv.at[chunk, step],
+            operand_send,
+            operand_recv.at[chunk],
             place(peer, gy),
         )
 
@@ -146,15 +142,15 @@
         return pltpu.make_async_copy(
             send.at[:, pl.ds(me * each + chunk * part, part)],
             held.at[:, channels(chunk), band(me), pl.ds(0, cols)],
-            own_sem.at[0, chunk],
+            operand_recv.at[chunk],
         )
 
     def pass_on(chunk):
         return remote(
             held.at[:, channels(chunk), :, pl.ds(0, cols)],
             held.at[:, channels(chunk), :, pl.ds(cols, cols)],
-            pass_send.at[chunk],
-            pass_recv.at[chunk],
+            pass_send,
+            operand_recv.at[chunk],
             place(me, inner_plane),
         )
 
@@ -163,8 +159,8 @@
         return remote(
             send.at[:, pl.ds(peer * each + chunk * part, part)],
             held.at[:, channels(chunk), band(me), pl.ds(cols, cols)],
-            direct_send.at[chunk, step],
-            direct_recv.at[chunk, step],
+            operand_send,
+            operand_recv.at[chunk],
             place(peer, inner_plane),
         )
 
@@ -172,18 +168,18 @@
         return remote(
             given.at[channels(chunk)],
             taken.at[channels(chunk)],
-            cross_send.at[chunk],
+            cross_send,
             cross_recv.at[chunk],
             place(me, 3 - gy),
         )
 
-    def hand_back(chunk, step, plane, side):
+    def hand_back(chunk, step, plane):
         peer = lax.rem(me + step, nr)
         return remote(
             taken.at[channels(chunk), band(peer), columns(plane)],
             out.at[pl.ds(me * each + chunk * part, part)],
-            back_send.at[side, chunk, step],
-            back_recv.at[chunk, step],
+            back_send,
+            back_recv,
             place(peer, plane),
         )
 
@@ -191,7 +187,7 @@
         return pltpu.make_async_copy(
             taken.at[channels(chunk), band(me), columns(inner_plane)],
             out.at[pl.ds(me * each + chunk * part, part)],
-            own_sem.at[1, chunk],
+            back_recv,
         )
 
     def load(block):
@@ -214,10 +210,12 @@
             device_id=place(peer % nr, peer // nr),
             device_id_type=pl.DeviceIdType.MESH,
         )
-    def dealt(chunk):
-        for step in range(1, nr):
-            deal(chunk, step).wait_recv()
-        keep_in(chunk).wait()
+
+    def take(ref, semaphore):
+        pltpu.make_async_copy(ref, ref, semaphore).wait()
+
+    def dealt(chunk, planes):
+        take(held.at[:, channels(chunk), :, pl.ds(0, planes * cols)], operand_recv.at[chunk])
 
     def product(channel, which):
         below = pl.ds(pl.multiple_of(which * 2 * cols, 2 * cols), 2 * cols)
@@ -292,7 +290,7 @@
 
             @pl.when(outer)
             def _():
-                dealt(DIRECT + group - 1)
+                dealt(DIRECT + group - 1, 1)
                 pass_on(DIRECT + group - 1).start()
 
     def store_gate(block):
@@ -326,25 +324,14 @@
     def _():
         @pl.loop(DIRECT + GROUPS - 1, chunks)
         def _(chunk):
-            dealt(chunk)
+            dealt(chunk, 1)
             pass_on(chunk).start()
             gate_turn(chunk)
 
-        @pl.loop(0, chunks)
-        def _(chunk):
-            for step in range(nr):
-                hand_back(chunk, step, outer_plane, 1).wait_recv()
-
-            @pl.when(chunk < DIRECT)
-            def _():
-                for step in range(nr):
-                    deal_inward(chunk, step).wait_send()
-
-            @pl.when(chunk >= DIRECT)
-            def _():
-                for step in range(1, nr):
-                    deal(chunk, step).wait_send()
-                pass_on(chunk).wait_send()
+        take(out, back_recv)
+        late = each - DIRECT * part
+        take(send.at[:, pl.ds(0, nr * DIRECT * part + (nr - 1) * late)], operand_send)
+        take(held.at[:, pl.ds(0, late), :, pl.ds(0, cols)], pass_send)
 
     @pl.when(inner)
     def _():
@@ -352,17 +339,7 @@
         def _(turn):
             @pl.when(turn < chunks)
             def _():
-                dealt(turn)
-
-                @pl.when(turn < DIRECT)
-                def _():
-                    for step in range(nr):
-                        deal_inward(turn, step).wait_recv()
-
-                @pl.when(turn >= DIRECT)
-                def _():
-                    pass_on(turn).wait_recv()
-
+                dealt(turn, 2)
 
                 @pl.loop(turn * part, (turn + 1) * part)
                 def _(channel):
@@ -381,23 +358,17 @@
                     taken[channel] = total.astype(jnp.bfloat16)
 
                 for step in range(nr):
-                    hand_back(chunk, step, outer_plane, 1).start()
+                    hand_back(chunk, step, outer_plane).start()
                 for step in range(1, nr):
-                    hand_back(chunk, step, inner_plane, 0).start()
+                    hand_back(chunk, step, inner_plane).start()
                 keep_out(chunk).start()
 
             gate_turn(turn)
 
-        @pl.loop(0, chunks)
-        def _(chunk):
-            for step in range(1, nr):
-                hand_back(chunk, step, inner_plane, 0).wait_recv()
-                hand_back(chunk, step, inner_plane, 0).wait_send()
-                deal(chunk, step).wait_send()
-            for step in range(nr):
-                hand_back(chunk, step, outer_plane, 1).wait_send()
-            cross(chunk).wait_send()
-            keep_out(chunk).wait()
+        take(out, back_recv)
+        take(send.at[:, pl.ds(0, (nr - 1) * each)], operand_send)
+        take(given, cross_send)
+        take(taken.at[:, pl.ds(0, (2 * nr - 1) * rows // 2)], back_send)
 
 
 def upright(row):
@@ -451,19 +422,15 @@
             pltpu.VMEM((2, each, side, 2 * tile_cols), jnp.bfloat16),
             pltpu.VMEM((each, side, 2 * tile_cols), jnp.bfloat16),
             pltpu.VMEM((each, side, 2 * tile_cols), jnp.bfloat16),
-            dma((CHUNKS, nr)),
-            dma((CHUNKS, nr)),
+            dma,
             dma((CHUNKS,)),
+            dma,
+            dma,
             dma((CHUNKS,)),
-            dma((CHUNKS,)),
-            dma((CHUNKS,)),
-            dma((2, CHUNKS, nr)),
-            dma((CHUNKS, nr)),
-            dma((2, CHUNKS)),
+            dma,
+            dma,
             dma((steps,)),
             dma((2,)),
-            dma((DIRECT, nr)),
-            dma((DIRECT, nr)),
         ],
         compiler_params=pltpu.CompilerParams(
             collective_id=0, has_side_effects=True, vmem_limit_bytes=63 * 2**20

time: 227 us -> 220 us (0.969)
  Pallas kernels: 226 us -> 219 us
    pallas_call x1, Pallas kernels: 216 us -> 209 us  [channel_body(): pl.pallas_call(functools.partial(exchange_kernel, nx, nz), name='exchange...]
where the time goes in v1:
time: 220 us
  Pallas kernels  219 us (100%)
    pallas_call x1, Pallas kernels, channel_body(): pl.pallas_call(functools.partial(exchange_kernel, nx, nz), name='exchange...  209 us
    pallas_call x1, Pallas kernels, channel_body(): pl.pallas_call(finish_kernel, name='finish', grid=(steps,), out_shape=jax...  10.3 us

profile of v1, /device:TPU:0, one launch (start us, length us, event | category | flops | bytes accessed | tf_op | source)
XLA Modules:
  0.0 219.8 jit_solution(16888758185283024767)
XLA Ops:
  0.7 208.9 %exchange.1 = (bf16[128,128,128]{2,1,0:T(8,128)(2,1)}, f32[128,128,128]{2,1,0:T(8,128)}) custom-call(s32[1]{0:T(128)S(6)} %copy.10.lengths, bf16[128,128,128]{2,1,0:T(8,128)(2,1)} %pair.1, f32[1,128]{1,0:T(1,128)} %bitcast.4, f32[1,128]{1,0:T(1,128)} %bitcast.5, bf16[128,512]{1,0:T(8,128)(2,1)} %w_ab.1, bf16[128,128]{1,0:T(8,128)(2,1)} %w_gate.1), custom_call_target="tpu_custom_call" | custom-call | tf_op jit(solution)/shard_map/exchange/pallas_call | solution.py:409
  209.5 10.3 %finish.1 = bf16[128,128,128]{2,1,0:T(8,128)(2,1)} custom-call(f32[128,128,128]{2,1,0:T(8,128)} %get-tuple-element.7.gate, bf16[128,128,128]{2,1,0:T(8,128)(2,1)} %get-tuple-element.8.tri, f32[1,128]{1,0:T(1,128)} %bitcast.6, f32[1,128]{1,0:T(1,128)} %bitcast.7, bf16[128,128]{1,0:T(8,128)(2,1)} %w_out.1), custom_call_target="tpu_custom_call" | custom-call | tf_op jit(solution)/shard_map/finish/pallas_call | solution.py:439
